TPU v7x, 128 devices: a whole 4x4x4 slice. The times are simulated.
128 devices in a mesh: tm: 8 (over z, core), rows: 16 (over x, y).
Axes of the slice: x: 4, y: 4, z: 4, core: 2. Of those that a mesh axis runs over, the one named last changes fastest.
Arguments:
- feat_mid: bfloat16 [32, 128, 128, 256], P('tm', 'rows'), may hold values from -15 to 15
- gain_mid: float32 [256], replicated, may hold values from 0.1 to 1.9
- conv_mid: bfloat16 [3, 3, 3, 256, 256], replicated, may hold values from -0.078125 to 0.078125
- down_weight: bfloat16 [8, 256, 512], replicated, may hold values from -0.125 to 0.125
- wavelets: bfloat16 [16, 24, 64, 64], P('tm', None, 'rows'), may hold values from -6 to 6
- inject_weight: bfloat16 [24, 512], replicated, may hold values from -1.25 to 1.25
- gain_deep: float32 [512], replicated, may hold values from 0.1 to 1.9
- conv_deep: bfloat16 [3, 3, 3, 512, 512], replicated, may hold values from -0.0546875 to 0.0546875
Outputs:
- encoded: bfloat16 [16, 64, 64, 512], P('tm', 'rows')
All inputs are finite; a program needn't handle non-finite values.
Results may differ from a plain program's by a relative error of at most 0.0095.
Values may be sent and summed in bfloat16 or wider, within the bound.
A program may use at most 256 MiB of HBM per device.

v0:
```python
import jax
import jax.numpy as jnp
from jax import lax
from jax.sharding import PartitionSpec as P

epsilon = 1e-06
haar_scale = 0.35355339059327373


def passed_along(block, axis, distance):
    devices = range(lax.axis_size(axis))
    route = [(i - distance, i) for i in devices if i - distance in devices]
    return lax.ppermute(block, axis, route)


def padded_2(block, sides, width):
    for axis, dim in sides:
        count = lax.axis_size(axis)
        forward = [(i, i + 1) for i in range(count - 1)]
        backward = [(target, source) for source, target in forward]
        low = lax.ppermute(
            lax.slice_in_dim(block, block.shape[dim] - width, None, axis=dim), axis, forward
        )
        high = lax.ppermute(lax.slice_in_dim(block, 0, width, axis=dim), axis, backward)
        block = jnp.concatenate([low, block, high], axis=dim)
    return block


def norm_act(values, scales):
    average = jnp.mean(values, axis=-1, keepdims=True)
    centred = values - average
    spread = jnp.mean(centred * centred, axis=-1, keepdims=True)
    return jax.nn.silu(centred * lax.rsqrt(spread + epsilon) * scales).astype(jnp.bfloat16)


def causal_taps(padded, weight, frames, row_count, breadth):
    padded = jnp.pad(padded, ((0, 0), (0, 0), (1, 1), (0, 0)))
    summed = jnp.zeros((frames, row_count, breadth, weight.shape[-1]), jnp.float32)
    for depth_tap in range(3):
        for row_tap in range(3):
            for col_tap in range(3):
                window = padded[
                    depth_tap : depth_tap + frames,
                    row_tap : row_tap + row_count,
                    col_tap : col_tap + breadth,
                ]
                summed = summed + jnp.einsum(
                    "fhwc,cd->fhwd",
                    window,
                    weight[depth_tap, row_tap, col_tap],
                    preferred_element_type=jnp.float32,
                )
    return summed


def butterfly(blocks, which_axis):
    leading = lax.index_in_dim(blocks, 0, which_axis, keepdims=False)
    trailing = lax.index_in_dim(blocks, 1, which_axis, keepdims=False)
    return (leading + trailing, leading - trailing)


def haar_project(level_two, down_weight):
    frames, height, breadth, channels = level_two.shape
    blocks = level_two.astype(jnp.float32).reshape(
        frames // 2, 2, height // 2, 2, breadth // 2, 2, channels
    )
    projected = jnp.zeros(
        (frames // 2 * (height // 2) * (breadth // 2), down_weight.shape[-1]), jnp.float32
    )
    band_index = 0
    for time_part in butterfly(blocks, 1):
        for row_part in butterfly(time_part, 2):
            for col_part in butterfly(row_part, 3):
                subband = (col_part * haar_scale).astype(jnp.bfloat16).reshape(-1, channels)
                projected = projected + jnp.dot(
                    subband, down_weight[band_index], preferred_element_type=jnp.float32
                )
                band_index = band_index + 1
    return projected.reshape(frames // 2, height // 2, breadth // 2, -1)


def on_device(
    feat_mid, gain_mid, conv_mid, down_weight, wavelets, inject_weight, gain_deep, conv_deep
):
    frames, row_count, breadth, channels = feat_mid.shape
    normed = norm_act(feat_mid.astype(jnp.float32), gain_mid)
    cached = passed_along(normed[frames - 2 :], "tm", 1)
    padded = padded_2(jnp.concatenate([cached, normed], 0), (("rows", 1),), 1)
    conv_out = causal_taps(padded, conv_mid, frames, row_count, breadth)
    level_two = (feat_mid.astype(jnp.float32) + conv_out).astype(jnp.bfloat16)
    injected = jnp.einsum(
        "fbhw,bd->fhwd", wavelets, inject_weight, preferred_element_type=jnp.float32
    )
    feat_deep = haar_project(level_two, down_weight) + injected
    normed_deep = norm_act(feat_deep, gain_deep)
    deep_frames = frames // 2
    deep_rows_count = row_count // 2
    deep_breadth = breadth // 2
    cached_deep = passed_along(normed_deep, "tm", 1)
    padded_deep = padded_2(jnp.concatenate([cached_deep, normed_deep], 0), (("rows", 1),), 1)
    conv_deep_out = causal_taps(padded_deep, conv_deep, deep_frames, deep_rows_count, deep_breadth)
    return (feat_deep + conv_deep_out).astype(jnp.bfloat16)


def solution(mesh):
    return jax.shard_map(
        on_device,
        mesh=mesh,
        in_specs=(
            P("tm", "rows", None, None),
            P(),
            P(),
            P(),
            P("tm", None, "rows", None),
            P(),
            P(),
            P(),
        ),
        out_specs=P("tm", "rows", None, None),
        check_vma=False,
    )
```

profile of v0, /device:TPU:70, one launch (start us, length us, event | category | flops | bytes accessed | tf_op | source)
XLA Modules:
  0.0 195.4 jit_solution(4942520749688028642)
XLA Ops:
  7.5 2.7 %fusion.210 = f32[4,8,128,256]{3,2,1,0:T(8,128)} fusion(bf16[4,8,128,256]{3,2,1,0:T(8,128)(2,1)S(1)} %fusion.10, bf16[3,3,3,256,256]{4,3,2,1,0:T(8,128)(2,1)S(1)} %copy-done.3), kind=kOutput, calls=%fused_computation.252 | convolution fusion | flops 536870912 | bytes 6422528 | tf_op jit(solution)/shard_map/fhwc,cd->fhwd/dot_general | solution.py:47
  10.2 11.5 %collective-permute-done = bf16[2,8,128,256]{3,2,1,0:T(8,128)(2,1)S(1)} collective-permute-done((bf16[2,8,128,256]{3,2,1,0:T(8,128)(2,1)S(1)}, bf16[2,8,128,256]{3,2,1,0:T(8,128)(2,1)S(1)}, u32[]{:S(2)}, u32[]{:S(2)}) %collective-permute-start) | collective-permute-done | bytes 1048608 | tf_op jit(solution)/shard_map/ppermute | solution.py:13
  21.7 3.5 %collective-permute-start.1 = (bf16[6,1,128,256]{3,2,1,0:T(8,128)(2,1)S(1)}, bf16[6,1,128,256]{3,2,1,0:T(8,128)(2,1)S(1)}, u32[]{:S(2)}, u32[]{:S(2)}) collective-permute-start(bf16[6,1,128,256]{3,2,1,0:T(8,128)(2,1)S(1)} %get-tuple-element.9), channel_id=1, source_target_pairs={{0,1},{1,2},{2,3},{3,4},{4,5},{5,6},{6,7},{7,8},{8,9},{9,10},{10,1... | collective-permute-start | bytes 1179656 | tf_op jit(solution)/shard_map/ppermute | solution.py:21
  25.2 4.5 %collective-permute-start.2 = (bf16[6,1,128,256]{3,2,1,0:T(8,128)(2,1)S(1)}, bf16[6,1,128,256]{3,2,1,0:T(8,128)(2,1)S(1)}, u32[]{:S(2)}, u32[]{:S(2)}) collective-permute-start(bf16[6,1,128,256]{3,2,1,0:T(8,128)(2,1)S(1)} %get-tuple-element.10), channel_id=1, source_target_pairs={{1,0},{2,1},{3,2},{4,3},{5,4},{6,5},{7,6},{8,7},{9,8},{10,9},{11,1... | collective-permute-start | bytes 1179656 | tf_op jit(solution)/shard_map/ppermute | solution.py:24
  37.2 3.4 %select_maximum_fusion = bf16[6,10,130,256]{3,2,1,0:T(8,128)(2,1)S(1)} fusion(bf16[6,1,128,256]{3,2,1,0:T(8,128)(2,1)S(1)} %collective-permute-done.2, bf16[6,1,128,256]{3,2,1,0:T(8,128)(2,1)S(1)} %collective-permute-done.1, bf16[4,8,128,256]{3,2,1,0:T(8,128)(2,1)S(1)} %fusion.10, bf16[2,8,128,256]{3,2,1,0:T(8,128)(2,1)S(1)} %collective-permute-done), kind=kLoop, calls=%fused_computation.19 | loop fusion | flops 29952000 | bytes 7925760 | tf_op jit(solution)/shard_map/concatenate | solution.py:25
  40.6 3.0 %fusion.20 = f32[4,8,128,256]{3,2,1,0:T(8,128)} fusion(bf16[6,10,130,256]{3,2,1,0:T(8,128)(2,1)S(1)} %select_maximum_fusion, bf16[3,3,3,256,256]{4,3,2,1,0:T(8,128)(2,1)S(1)} %copy-done.3), kind=kOutput, calls=%fused_computation.30 | convolution fusion | flops 536870912 | bytes 6422528 | tf_op jit(solution)/shard_map/fhwc,cd->fhwd/dot_general | solution.py:47
  43.6 2.7 %fusion.22 = f32[4,8,128,256]{3,2,1,0:T(8,128)} fusion(bf16[6,10,130,256]{3,2,1,0:T(8,128)(2,1)S(1)} %select_maximum_fusion, bf16[3,3,3,256,256]{4,3,2,1,0:T(8,128)(2,1)S(1)} %copy-done.3), kind=kOutput, calls=%fused_computation.32 | convolution fusion | flops 536870912 | bytes 6422528 | tf_op jit(solution)/shard_map/fhwc,cd->fhwd/dot_general | solution.py:47
  51.6 2.7 %fusion.28 = f32[4,8,128,256]{3,2,1,0:T(8,128)} fusion(bf16[6,10,130,256]{3,2,1,0:T(8,128)(2,1)S(1)} %select_maximum_fusion, bf16[3,3,3,256,256]{4,3,2,1,0:T(8,128)(2,1)S(1)} %copy-done.3), kind=kOutput, calls=%fused_computation.38 | convolution fusion | flops 536870912 | bytes 6422528 | tf_op jit(solution)/shard_map/fhwc,cd->fhwd/dot_general | solution.py:47
  54.3 2.7 %fusion.30 = f32[4,8,128,256]{3,2,1,0:T(8,128)} fusion(bf16[6,10,130,256]{3,2,1,0:T(8,128)(2,1)S(1)} %select_maximum_fusion, bf16[3,3,3,256,256]{4,3,2,1,0:T(8,128)(2,1)S(1)} %copy-done.3), kind=kOutput, calls=%fused_computation.40 | convolution fusion | flops 536870912 | bytes 6422528 | tf_op jit(solution)/shard_map/fhwc,cd->fhwd/dot_general | solution.py:47
  57.0 2.8 %fusion.32 = f32[4,8,128,256]{3,2,1,0:T(8,128)} fusion(bf16[6,10,130,256]{3,2,1,0:T(8,128)(2,1)S(1)} %select_maximum_fusion, bf16[3,3,3,256,256]{4,3,2,1,0:T(8,128)(2,1)S(1)} %copy-done.3), kind=kOutput, calls=%fused_computation.42 | convolution fusion | flops 536870912 | bytes 6422528 | tf_op jit(solution)/shard_map/fhwc,cd->fhwd/dot_general | solution.py:47
  59.8 2.7 %fusion.34 = f32[4,8,128,256]{3,2,1,0:T(8,128)} fusion(bf16[6,10,130,256]{3,2,1,0:T(8,128)(2,1)S(1)} %select_maximum_fusion, bf16[3,3,3,256,256]{4,3,2,1,0:T(8,128)(2,1)S(1)} %copy-done.3), kind=kOutput, calls=%fused_computation.44 | convolution fusion | flops 536870912 | bytes 6422528 | tf_op jit(solution)/shard_map/fhwc,cd->fhwd/dot_general | solution.py:47
  65.1 2.8 %fusion.38 = f32[4,8,128,256]{3,2,1,0:T(8,128)} fusion(bf16[6,10,130,256]{3,2,1,0:T(8,128)(2,1)S(1)} %select_maximum_fusion, bf16[3,3,3,256,256]{4,3,2,1,0:T(8,128)(2,1)S(1)} %copy-done.3), kind=kOutput, calls=%fused_computation.48 | convolution fusion | flops 536870912 | bytes 6422528 | tf_op jit(solution)/shard_map/fhwc,cd->fhwd/dot_general | solution.py:47
  75.9 2.7 %fusion.46 = f32[4,8,128,256]{3,2,1,0:T(8,128)} fusion(bf16[6,10,130,256]{3,2,1,0:T(8,128)(2,1)S(1)} %select_maximum_fusion, bf16[3,3,3,256,256]{4,3,2,1,0:T(8,128)(2,1)S(1)} %copy-done.3), kind=kOutput, calls=%fused_computation.56 | convolution fusion | flops 536870912 | bytes 6422528 | tf_op jit(solution)/shard_map/fhwc,cd->fhwd/dot_general | solution.py:47
  78.7 2.7 %fusion.48 = f32[4,8,128,256]{3,2,1,0:T(8,128)} fusion(bf16[6,10,130,256]{3,2,1,0:T(8,128)(2,1)S(1)} %select_maximum_fusion, bf16[3,3,3,256,256]{4,3,2,1,0:T(8,128)(2,1)S(1)} %copy-done.3), kind=kOutput, calls=%fused_computation.58 | convolution fusion | flops 536870912 | bytes 6422528 | tf_op jit(solution)/shard_map/fhwc,cd->fhwd/dot_general | solution.py:47
  81.3 2.7 %fusion.50 = f32[4,8,128,256]{3,2,1,0:T(8,128)} fusion(bf16[6,10,130,256]{3,2,1,0:T(8,128)(2,1)S(1)} %select_maximum_fusion, bf16[3,3,3,256,256]{4,3,2,1,0:T(8,128)(2,1)S(1)} %copy-done.3), kind=kOutput, calls=%fused_computation.60 | convolution fusion | flops 536870912 | bytes 6422528 | tf_op jit(solution)/shard_map/fhwc,cd->fhwd/dot_general | solution.py:47
  84.0 2.7 %fusion.52 = f32[4,8,128,256]{3,2,1,0:T(8,128)} fusion(bf16[6,10,130,256]{3,2,1,0:T(8,128)(2,1)S(1)} %select_maximum_fusion, bf16[3,3,3,256,256]{4,3,2,1,0:T(8,128)(2,1)S(1)} %copy-done.3), kind=kOutput, calls=%fused_computation.62 | convolution fusion | flops 536870912 | bytes 6422528 | tf_op jit(solution)/shard_map/fhwc,cd->fhwd/dot_general | solution.py:47
  89.4 2.8 %fusion.206 = f32[4,8,128,256]{3,2,1,0:T(8,128)} fusion(bf16[3,3,3,256,256]{4,3,2,1,0:T(8,128)(2,1)S(1)} %copy-done.3, bf16[6,1,128,256]{3,2,1,0:T(8,128)(2,1)S(1)} %collective-permute-done.2, bf16[4,8,128,256]{3,2,1,0:T(8,128)(2,1)S(1)} %fusion.10, bf16[2,8,128,256]{3,2,1,0:T(8,128)(2,1)S(1)} %collective-permute-done), kind=kOutput, calls=%fused_computation.248 | convolution fusion | flops 547487744 | bytes 7864320 | tf_op jit(solution)/shard_map/fhwc,cd->fhwd/dot_general | solution.py:47
  92.2 2.7 %fusion.229 = f32[4,8,128,256]{3,2,1,0:T(8,128)} fusion(bf16[3,3,3,256,256]{4,3,2,1,0:T(8,128)(2,1)S(1)} %copy-done.3, bf16[6,1,128,256]{3,2,1,0:T(8,128)(2,1)S(1)} %collective-permute-done.2, bf16[4,8,128,256]{3,2,1,0:T(8,128)(2,1)S(1)} %fusion.10, bf16[2,8,128,256]{3,2,1,0:T(8,128)(2,1)S(1)} %collective-permute-done), kind=kOutput, calls=%fused_computation.271 | convolution fusion | flops 547487744 | bytes 7864320 | tf_op jit(solution)/shard_map/fhwc,cd->fhwd/dot_general | solution.py:47
  102.9 36.5 %fusion.56 = f32[4,8,128,256]{3,2,1,0:T(8,128)} fusion(bf16[6,10,130,256]{3,2,1,0:T(8,128)(2,1)} %copy-done.1, f32[4,8,128,256]{3,2,1,0:T(8,128)} %fusion.206, f32[4,8,128,256]{3,2,1,0:T(8,128)} %fusion.20, f32[4,8,128,256]{3,2,1,0:T(8,128)} %fusion.22, f32[4,8,128,256]{3,2,1,0:T(8,128)} %fusion.210, f32[4,8,128,256]{3,2,1,0:T(8,128)} %fusion.24, ...), kind=kOutput, calls=%fused_computation.68 | convolution fusion | flops 568328192 | bytes 117571584 | tf_op jit(solution)/shard_map/fhwc,cd->fhwd/dot_general | solution.py:47
  139.4 5.8 %reshape.77 = f32[2,2,4,2,64,2,256]{6,5,4,3,2,1,0:T(2,128)} reshape(f32[4,8,128,256]{3,2,1,0:T(8,128)} %fusion.56) | data formatting | bytes 8388608 | tf_op jit(solution)/shard_map/reshape | solution.py:64
  145.3 3.7 %fusion.271 = (f32[2,1,4,2,64,2,256]{6,5,4,3,2,1,0:T(2,128)S(1)}, f32[2,1,4,2,64,2,256]{6,5,4,3,2,1,0:T(2,128)S(1)}) fusion(f32[2,2,4,2,64,2,256]{6,5,4,3,2,1,0:T(2,128)} %reshape.77), kind=kLoop, calls=%fused_computation.317 | loop fusion | bytes 8388608 | tf_op jit(solution)/shard_map/slice | solution.py:57
  159.2 7.1 %collective-permute-done.3 = bf16[2,4,64,512]{3,2,1,0:T(8,128)(2,1)S(1)} collective-permute-done((bf16[2,4,64,512]{3,2,1,0:T(8,128)(2,1)S(1)}, bf16[2,4,64,512]{3,2,1,0:T(8,128)(2,1)S(1)}, u32[]{:S(2)}, u32[]{:S(2)}) %collective-permute-start.3) | collective-permute-done | bytes 524320 | tf_op jit(solution)/shard_map/ppermute | solution.py:13
  166.3 3.4 %collective-permute-start.4 = (bf16[4,1,64,512]{3,2,1,0:T(8,128)(2,1)S(1)}, bf16[4,1,64,512]{3,2,1,0:T(8,128)(2,1)S(1)}, u32[]{:S(2)}, u32[]{:S(2)}) collective-permute-start(bf16[4,1,64,512]{3,2,1,0:T(8,128)(2,1)S(1)} %get-tuple-element.15), channel_id=1, source_target_pairs={{0,1},{1,2},{2,3},{3,4},{4,5},{5,6},{6,7},{7,8},{8,9},{9,10},{10,1... | collective-permute-start | bytes 786440 | tf_op jit(solution)/shard_map/ppermute | solution.py:21
  169.8 5.1 %collective-permute-start.5 = (bf16[4,1,64,512]{3,2,1,0:T(8,128)(2,1)S(1)}, bf16[4,1,64,512]{3,2,1,0:T(8,128)(2,1)S(1)}, u32[]{:S(2)}, u32[]{:S(2)}) collective-permute-start(bf16[4,1,64,512]{3,2,1,0:T(8,128)(2,1)S(1)} %get-tuple-element.16), channel_id=1, source_target_pairs={{1,0},{2,1},{3,2},{4,3},{5,4},{6,5},{7,6},{8,7},{9,8},{10,9},{11,1... | collective-permute-start | bytes 786440 | tf_op jit(solution)/shard_map/ppermute | solution.py:24
  (98 shorter events, 72.0 us)
Async XLA Ops:
  0.0 154.2 %copy-start = (bf16[24,512]{1,0:T(8,128)(2,1)S(1)}, bf16[24,512]{1,0:T(8,128)(2,1)}, u32[]{:S(2)}) copy-start(bf16[24,512]{1,0:T(8,128)(2,1)} %param.13) | copy-start | bytes 73732
  0.0 2.4 %copy-start.2 = (bf16[4,8,128,256]{3,2,1,0:T(8,128)(2,1)S(1)}, bf16[4,8,128,256]{3,2,1,0:T(8,128)(2,1)}, u32[]{:S(2)}) copy-start(bf16[4,8,128,256]{3,2,1,0:T(8,128)(2,1)} %param.8) | copy-start | bytes 6291460
  0.0 3.7 %copy-start.7 = (f32[256]{0:T(256)S(1)}, f32[256]{0:T(256)}, u32[]{:S(2)}) copy-start(f32[256]{0:T(256)} %param.9) | copy-start | bytes 3076
  3.7 3.8 %copy-start.3 = (bf16[3,3,3,256,256]{4,3,2,1,0:T(8,128)(2,1)S(1)}, bf16[3,3,3,256,256]{4,3,2,1,0:T(8,128)(2,1)}, u32[]{:S(2)}) copy-start(bf16[3,3,3,256,256]{4,3,2,1,0:T(8,128)(2,1)} %param.10) | copy-start | bytes 10616836
  5.5 16.1 %collective-permute-start = (bf16[2,8,128,256]{3,2,1,0:T(8,128)(2,1)S(1)}, bf16[2,8,128,256]{3,2,1,0:T(8,128)(2,1)S(1)}, u32[]{:S(2)}, u32[]{:S(2)}) collective-permute-start(bf16[2,8,128,256]{3,2,1,0:T(8,128)(2,1)S(1)} %slice.567), channel_id=1, source_target_pairs={{0,16},{16,32},{32,48},{48,64},{64,80},{80,96},{96,112},{1,17},{17... | collective-permute-start | bytes 3145736 | tf_op jit(solution)/shard_map/ppermute | solution.py:13
  21.7 14.3 %collective-permute-start.1 = (bf16[6,1,128,256]{3,2,1,0:T(8,128)(2,1)S(1)}, bf16[6,1,128,256]{3,2,1,0:T(8,128)(2,1)S(1)}, u32[]{:S(2)}, u32[]{:S(2)}) collective-permute-start(bf16[6,1,128,256]{3,2,1,0:T(8,128)(2,1)S(1)} %get-tuple-element.9), channel_id=1, source_target_pairs={{0,1},{1,2},{2,3},{3,4},{4,5},{5,6},{6,7},{7,8},{8,9},{9,10},{10,1... | collective-permute-start | bytes 1179656 | tf_op jit(solution)/shard_map/ppermute | solution.py:21
  25.2 12.0 %collective-permute-start.2 = (bf16[6,1,128,256]{3,2,1,0:T(8,128)(2,1)S(1)}, bf16[6,1,128,256]{3,2,1,0:T(8,128)(2,1)S(1)}, u32[]{:S(2)}, u32[]{:S(2)}) collective-permute-start(bf16[6,1,128,256]{3,2,1,0:T(8,128)(2,1)S(1)} %get-tuple-element.10), channel_id=1, source_target_pairs={{1,0},{2,1},{3,2},{4,3},{5,4},{6,5},{7,6},{8,7},{9,8},{10,9},{11,1... | collective-permute-start | bytes 1179656 | tf_op jit(solution)/shard_map/ppermute | solution.py:24
  40.6 43.5 %copy-start.1 = (bf16[6,10,130,256]{3,2,1,0:T(8,128)(2,1)}, bf16[6,10,130,256]{3,2,1,0:T(8,128)(2,1)S(1)}, u32[]{:S(2)}) copy-start(bf16[6,10,130,256]{3,2,1,0:T(8,128)(2,1)S(1)} %select_maximum_fusion) | copy-start | bytes 11980804
  150.1 1.6 copy-start.4
  152.6 27.2 %slice-start = ((s8[14155776]{0:T(1024)(128)(4,1)}), s8[4194304]{0:T(1024)(128)(4,1)S(1)}, s32[]{:S(2)}) async-start(s8[14155776]{0:T(1024)(128)(4,1)} %bitcast.444), calls=%async_computation | async-start | bytes 8388608
  153.2 1.1 copy-start.5
  153.3 26.5 %slice-start.1 = ((s8[14155776]{0:T(1024)(128)(4,1)}), s8[4194304]{0:T(1024)(128)(4,1)S(1)}, s32[]{:S(2)}) async-start(s8[14155776]{0:T(1024)(128)(4,1)} %bitcast.444), calls=%async_computation.1 | async-start | bytes 8388608
  153.9 1.3 copy-start.6
  154.4 25.5 %slice-start.2 = ((s8[14155776]{0:T(1024)(128)(4,1)}), s8[4194304]{0:T(1024)(128)(4,1)S(1)}, s32[]{:S(2)}) async-start(s8[14155776]{0:T(1024)(128)(4,1)} %bitcast.444), calls=%async_computation.2 | async-start | bytes 8388608
  155.5 10.8 %collective-permute-start.3 = (bf16[2,4,64,512]{3,2,1,0:T(8,128)(2,1)S(1)}, bf16[2,4,64,512]{3,2,1,0:T(8,128)(2,1)S(1)}, u32[]{:S(2)}, u32[]{:S(2)}) collective-permute-start(bf16[2,4,64,512]{3,2,1,0:T(8,128)(2,1)S(1)} %multiply_convert_fusion), channel_id=1, source_target_pairs={{0,16},{16,32},{32,48},{48,64},{64,80},{80,96},{96,112},{1,17},{17... | collective-permute-start | bytes 1572872 | tf_op jit(solution)/shard_map/ppermute | solution.py:13
  166.3 11.5 %collective-permute-start.4 = (bf16[4,1,64,512]{3,2,1,0:T(8,128)(2,1)S(1)}, bf16[4,1,64,512]{3,2,1,0:T(8,128)(2,1)S(1)}, u32[]{:S(2)}, u32[]{:S(2)}) collective-permute-start(bf16[4,1,64,512]{3,2,1,0:T(8,128)(2,1)S(1)} %get-tuple-element.15), channel_id=1, source_target_pairs={{0,1},{1,2},{2,3},{3,4},{4,5},{5,6},{6,7},{7,8},{8,9},{9,10},{10,1... | collective-permute-start | bytes 786440 | tf_op jit(solution)/shard_map/ppermute | solution.py:21
  169.8 10.0 %slice-start.3 = ((s8[14155776]{0:T(1024)(128)(4,1)}), s8[1572864]{0:T(1024)(128)(4,1)S(1)}, s32[]{:S(2)}) async-start(s8[14155776]{0:T(1024)(128)(4,1)} %bitcast.444), calls=%async_computation.3 | async-start | bytes 3145728
  169.8 9.0 %collective-permute-start.5 = (bf16[4,1,64,512]{3,2,1,0:T(8,128)(2,1)S(1)}, bf16[4,1,64,512]{3,2,1,0:T(8,128)(2,1)S(1)}, u32[]{:S(2)}, u32[]{:S(2)}) collective-permute-start(bf16[4,1,64,512]{3,2,1,0:T(8,128)(2,1)S(1)} %get-tuple-element.16), channel_id=1, source_target_pairs={{1,0},{2,1},{3,2},{4,3},{5,4},{6,5},{7,6},{8,7},{9,8},{10,9},{11,1... | collective-permute-start | bytes 786440 | tf_op jit(solution)/shard_map/ppermute | solution.py:24
where the time goes:
time: 199 us; the launch traced here: 195 us
  matrix products  129 us (65%)
  waiting for transfers between devices  21.7 us (11%)
  starting transfers between devices  20.6 us (10%)
  other arithmetic  12.2 us (6%)
  local copies, waits for them, and re-layouts  10.9 us (5%)
    dot_general x54, matrix products, causal_taps(): jnp.einsum('fhwc,cd->fhwd', window, weight[depth_tap, row_tap, col_tap],...  127 us
    ppermute x2, waiting for transfers between devices, passed_along(): return lax.ppermute(block, axis, route)  18.6 us
    ppermute x2, starting transfers between devices, padded_2(): lax.ppermute(lax.slice_in_dim(block, 0, width, axis=dim), axis, backward)  9.57 us
    ppermute x2, starting transfers between devices, padded_2(): lax.ppermute(lax.slice_in_dim(block, block.shape[dim] - width, None, axis...  6.93 us
    reshape x1, local copies, waits for them, and re-layouts, haar_project(): level_two.astype(jnp.float32)  5.84 us
    concatenate x2, other arithmetic, padded_2(): block = jnp.concatenate([low, block, high], axis=dim)  4.36 us
    ppermute x2, starting transfers between devices, passed_along(): return lax.ppermute(block, axis, route)  4.1 us
  transfers between devices with their start and end apart: 6, of which 5 were waited for; matrix products, arithmetic and copies ran while one was open for 6% of the time, Pallas kernels for 0%

commit v1 on v0

v1 whole, which is shorter than its diff:
```python
import functools

import jax
import jax.numpy as jnp
from jax import lax
from jax.experimental import pallas as pl
from jax.experimental.pallas import tpu as pltpu
from jax.sharding import PartitionSpec as P

epsilon = 1e-06
haar_scale = 0.35355339059327373
MESH = pl.DeviceIdType.MESH
BF = jnp.bfloat16
F32 = jnp.float32


def norm_silu(x, half_gain):
    mean = jnp.mean(x, axis=-1, keepdims=True)
    c = x - mean
    var = jnp.mean(c * c, axis=-1, keepdims=True)
    h = c * lax.rsqrt(var + epsilon) * half_gain
    return (h + h * jnp.tanh(h)).astype(BF)


def shift_down(x):
    row = lax.broadcasted_iota(jnp.int32, x.shape, 0)
    return jnp.where(row == 0, 0.0, pltpu.roll(x, 1, 0))


def shift_up(x):
    n = x.shape[0]
    row = lax.broadcasted_iota(jnp.int32, x.shape, 0)
    return jnp.where(row == n - 1, 0.0, pltpu.roll(x, n - 1, 0))


def kernel(
    n_tm, n_rows,
    feat, gain_mid, conv_mid, down, wav, inj, gain_deep, conv_deep,
    out,
    fv, wm, wdn, wd, wv, iv, injw, wavt, xp, ym, lv, sb, fd, yp, yd, ov,
    lsem, send, recv, osem,
    *accs,
):
    t_id, r_id = lax.axis_index("tm"), lax.axis_index("rows")
    has_prev, has_next = t_id > 0, t_id < n_tm - 1
    has_up, has_dn = r_id > 0, r_id < n_rows - 1
    acc = (accs[:6], accs[6:])

    def load(i, src, dst):
        return pltpu.make_async_copy(src, dst, lsem.at[i])

    feat_loads = [load(i, feat.at[i], fv.at[i]) for i in range(4)]
    for i in (3, 2, 1, 0):
        feat_loads[i].start()
    ld_wm = load(4, conv_mid, wm)
    ld_dn = load(5, down, wdn)
    ld_wv = load(6, wav, wv)
    ld_iv = load(7, inj, iv)
    ld_wd = load(8, conv_deep, wd)
    for ld in (ld_wm, ld_wv, ld_iv, ld_dn, ld_wd):
        ld.start()

    barrier = pltpu.get_barrier_semaphore()
    count = jnp.int32(0)
    for dt in (-1, 0, 1):
        for dr in (-1, 0, 1):
            if dt == 0 and dr == 0:
                continue
            there = jnp.bool_(True)
            if dt:
                there = has_prev if dt < 0 else has_next
            if dr:
                there_r = has_up if dr < 0 else has_dn
                there = jnp.logical_and(there, there_r) if dt else there_r
            count = count + there.astype(jnp.int32)

            @pl.when(there)
            def _():
                pl.semaphore_signal(
                    barrier, inc=1, device_id=(t_id + dt, r_id + dr), device_id_type=MESH
                )

    halo = {}

    def both(dt, dr):
        cond = {-1: (has_prev, has_up), 1: (has_next, has_dn)}
        target, source = None, None
        if dt:
            target, source = cond[dt][0], cond[-dt][0]
        if dr:
            tr, sr = cond[dr][1], cond[-dr][1]
            target = tr if target is None else jnp.logical_and(target, tr)
            source = sr if source is None else jnp.logical_and(source, sr)
        return target, source

    def add_halo(name, src, dst, dt, dr):
        i = len(halo)
        desc = pltpu.make_async_remote_copy(
            src_ref=src, dst_ref=dst, send_sem=send.at[i], recv_sem=recv.at[i],
            device_id=(t_id + dt, r_id + dr), device_id_type=MESH,
        )
        target, source = both(dt, dr)
        halo[name] = (desc, target, source)

    add_halo("u23", xp.at[4:6, 1], xp.at[4:6, 9], 0, -1)
    add_halo("d23", xp.at[4:6, 8], xp.at[4:6, 0], 0, 1)
    add_halo("u01", xp.at[2:4, 1], xp.at[2:4, 9], 0, -1)
    add_halo("d01", xp.at[2:4, 8], xp.at[2:4, 0], 0, 1)
    add_halo("z3", xp.at[5, 1:9], xp.at[1, 1:9], 1, 0)
    add_halo("z2", xp.at[4, 1:9], xp.at[0, 1:9], 1, 0)
    add_halo("zu", xp.at[4:6, 1], xp.at[0:2, 9], 1, -1)
    add_halo("zd", xp.at[4:6, 8], xp.at[0:2, 0], 1, 1)
    for f in (1, 0):
        add_halo(f"yu{f}", yp.at[2 + f, 1], yp.at[2 + f, 5], 0, -1)
        add_halo(f"yd{f}", yp.at[2 + f, 4], yp.at[2 + f, 0], 0, 1)
        add_halo(f"yz{f}", yp.at[2 + f, 1:5], yp.at[f, 1:5], 1, 0)
        add_halo(f"yzu{f}", yp.at[2 + f, 1], yp.at[f, 5], 1, -1)
        add_halo(f"yzd{f}", yp.at[2 + f, 4], yp.at[f, 0], 1, 1)

    def start(*names):
        for name in names:
            desc, target, _ = halo[name]
            pl.when(target)(desc.start)

    def arrive(*names):
        for name in names:
            desc, _, source = halo[name]
            pl.when(source)(desc.wait_recv)

    @pl.when(jnp.logical_not(has_prev))
    def _():
        xp[0:2] = jnp.zeros((2, 10, 128, 256), BF)
        yp[0:2] = jnp.zeros((2, 6, 64, 512), BF)

    @pl.when(jnp.logical_not(has_up))
    def _():
        xp[:, 0] = jnp.zeros((6, 128, 256), BF)
        yp[:, 0] = jnp.zeros((4, 64, 512), BF)

    @pl.when(jnp.logical_not(has_dn))
    def _():
        xp[:, 9] = jnp.zeros((6, 128, 256), BF)
        yp[:, 5] = jnp.zeros((4, 64, 512), BF)

    half_gain = gain_mid[...] * 0.5

    def norm_frame(f):
        feat_loads[f].wait()

        @pl.loop(0, 8)
        def _(r):
            for piece in range(2):
                rows = pl.ds(piece * 64, 64)
                xp[f + 2, r + 1, rows, :] = norm_silu(fv[f, r, rows, :].astype(F32), half_gain)

    norm_frame(3)
    norm_frame(2)
    pl.semaphore_wait(barrier, count)
    start("u23", "d23", "z3", "z2", "zu", "zd")
    norm_frame(1)
    norm_frame(0)
    start("u01", "d01")

    injw[...] = jnp.zeros((256, 512), BF)
    wavt[...] = jnp.zeros((2, 256, 256), BF)
    ld_wv.wait()
    ld_iv.wait()
    injw[0:24, :] = iv[...]
    for t in range(2):
        coeffs = wv[t].astype(F32)
        for h in range(4):
            wavt[t, h * 64:(h + 1) * 64, 0:24] = coeffs[:, h, :].T.astype(BF)

    def mid_block(t, first_rows, slot):
        k = 0
        for c in range(3):
            for a in range(3):
                for b in range(3):
                    tap = (a * 3 + b) * 3 + c
                    for q in range(2):
                        pltpu.matmul_push_rhs(wm[tap], k % 2, q)
                        for h in range(2):
                            pltpu.matmul_acc_lhs(
                                acc[q][c * 2 + h], xp[t + a, first_rows[q] + b + h],
                                load_staged_rhs=k % 2 if h == 0 else None,
                            )
                    k += 1
            for q in range(2):
                for h in range(2):
                    ym[slot, q, h, c] = pltpu.matmul_pop(acc[q][c * 2 + h])

    def mid_combine(t, first_rows, slot):
        for q in range(2):
            for h in range(2):
                r = first_rows[q] + h
                for n in range(2):
                    lanes = pl.ds(n * 128, 128)
                    total = shift_down(ym[slot, q, h, 0, :, lanes]) + ym[slot, q, h, 1, :, lanes]
                    total = total + shift_up(ym[slot, q, h, 2, :, lanes])
                    level = (fv[t, r, :, lanes].astype(F32) + total).astype(BF)
                    lv[t % 2, n, r] = level.astype(F32)

    inner, outer = (2, 4), (0, 6)

    def mid_pair(t0, first_rows):
        for i in range(2):
            mid_block(t0 + i, first_rows, i)
            mid_combine(t0 + i, first_rows, i)

    half_gain_deep = gain_deep[...] * 0.5

    def deep_frame(t):
        @pl.loop(0, 4)
        def _(r):
            for piece in range(4):
                for n in range(2):
                    lanes = pl.ds(n * 128, 128)
                    v = {}
                    for i in range(2):
                        for j in range(2):
                            for k in range(2):
                                v[i, j, k] = lv[
                                    i, n, 2 * r + j, pl.ds(piece * 32 + k, 16, stride=2), :
                                ]
                    for axis in range(3):
                        w = {}
                        for key in v:
                            if key[axis] == 0:
                                other = key[:axis] + (1,) + key[axis + 1:]
                                w[key] = v[key] + v[other]
                                w[other] = v[key] - v[other]
                        v = w
                    for i in range(2):
                        for j in range(2):
                            for k in range(2):
                                s = 4 * i + 2 * j + k
                                row = pl.multiple_of(r * 64 + piece * 16, 16)
                                sb[s, pl.ds(row, 16), lanes] = (v[i, j, k] * haar_scale).astype(BF)

        for s in range(9):
            for q in range(2):
                cols = slice(q * 256, (q + 1) * 256)
                rhs = wdn[s, :, cols] if s < 8 else injw[:, cols]
                pltpu.matmul_push_rhs(rhs, s % 2, q)
                for h in range(2):
                    rows = slice(h * 128, (h + 1) * 128)
                    lhs = sb[s, rows, :] if s < 8 else wavt[t, rows, :]
                    pltpu.matmul_acc_lhs(acc[q][h], lhs, load_staged_rhs=s % 2 if h == 0 else None)
        for h in range(2):
            for q in range(2):
                fd[t, h * 128:(h + 1) * 128, q * 256:(q + 1) * 256] = pltpu.matmul_pop(acc[q][h])

        @pl.loop(0, 4)
        def _(r):
            for piece in range(2):
                rows = pl.ds(pl.multiple_of(r * 64 + piece * 32, 32), 32)
                yp[t + 2, r + 1, pl.ds(piece * 32, 32), :] = norm_silu(fd[t, rows, :], half_gain_deep)

    def start_deep(f):
        start(f"yu{f}", f"yd{f}", f"yz{f}", f"yzu{f}", f"yzd{f}")

    ld_wm.wait()
    mid_pair(2, inner)
    arrive("u23", "d23", "u01", "d01")
    mid_pair(2, outer)
    ld_dn.wait()
    deep_frame(1)
    start_deep(1)
    arrive("z3", "z2", "zu", "zd")
    mid_pair(0, inner)
    mid_pair(0, outer)
    deep_frame(0)
    start_deep(0)

    ld_wd.wait()

    def deep_conv(t, order, waits):
        k = 0
        for step, a in enumerate(order):
            arrive(*waits[step])
            for c in range(3):
                for b in range(3):
                    tap = (a * 3 + b) * 3 + c
                    for d in range(2):
                        depth = slice(d * 256, (d + 1) * 256)
                        for q in range(2):
                            pltpu.matmul_push_rhs(
                                wd[tap, depth, q * 256:(q + 1) * 256], k % 2, q
                            )
                            for h in range(2):
                                lhs = yp[t + a, b + 2 * h:b + 2 * h + 2, :, depth]
                                pltpu.matmul_acc_lhs(
                                    acc[q][c * 2 + h], lhs.reshape(128, 256),
                                    load_staged_rhs=k % 2 if h == 0 else None,
                                )
                        k += 1
                if step == 2:
                    for q in range(2):
                        for h in range(2):
                            yd[t, c, h * 128:(h + 1) * 128, q * 256:(q + 1) * 256] = (
                                pltpu.matmul_pop(acc[q][c * 2 + h])
                            )

    def deep_combine(t):
        for r in range(4):
            rows = slice(r * 64, (r + 1) * 64)
            for n in range(4):
                lanes = slice(n * 128, (n + 1) * 128)
                total = shift_down(yd[t, 0, rows, lanes]) + yd[t, 1, rows, lanes]
                total = total + shift_up(yd[t, 2, rows, lanes])
                ov[t, r, :, lanes] = (fd[t, rows, lanes] + total).astype(BF)

    deep_conv(1, (2, 0, 1), (("yu1", "yd1"), ("yz1", "yzu1", "yzd1"), ("yu0", "yd0")))
    deep_combine(1)
    store1 = pltpu.make_async_copy(ov.at[1], out.at[1], osem.at[1])
    store1.start()
    deep_conv(0, (1, 2, 0), ((), (), ("yz0", "yzu0", "yzd0")))
    deep_combine(0)
    store0 = pltpu.make_async_copy(ov.at[0], out.at[0], osem.at[0])
    store0.start()

    for desc, target, _ in halo.values():
        pl.when(target)(desc.wait_send)
    store1.wait()
    store0.wait()


def on_device(n_tm, n_rows, feat, gain_mid, conv_mid, down, wav, inj, gain_deep, conv_deep):
    def body(*refs):
        def inner(*accs):
            kernel(n_tm, n_rows, *refs, *accs)

        pl.run_scoped(inner, *[pltpu.ACC(q)((128, 256), F32) for q in range(2) for _ in range(6)])

    hbm = pl.BlockSpec(memory_space=pl.ANY)
    vmem = pl.BlockSpec(memory_space=pltpu.VMEM)
    return pl.pallas_call(
        body,
        out_shape=jax.ShapeDtypeStruct((2, 4, 64, 512), BF),
        in_specs=[hbm, vmem, hbm, hbm, hbm, hbm, vmem, hbm],
        out_specs=hbm,
        scratch_shapes=[
            pltpu.VMEM((4, 8, 128, 256), BF),
            pltpu.VMEM((27, 256, 256), BF),
            pltpu.VMEM((8, 256, 512), BF),
            pltpu.VMEM((27, 512, 512), BF),
            pltpu.VMEM((2, 24, 4, 64), BF),
            pltpu.VMEM((24, 512), BF),
            pltpu.VMEM((256, 512), BF),
            pltpu.VMEM((2, 256, 256), BF),
            pltpu.VMEM((6, 10, 128, 256), BF),
            pltpu.VMEM((2, 2, 2, 3, 128, 256), F32),
            pltpu.VMEM((2, 2, 8, 128, 128), F32),
            pltpu.VMEM((8, 256, 256), BF),
            pltpu.VMEM((2, 256, 512), F32),
            pltpu.VMEM((4, 6, 64, 512), BF),
            pltpu.VMEM((2, 3, 256, 512), F32),
            pltpu.VMEM((2, 4, 64, 512), BF),
            pltpu.SemaphoreType.DMA((9,)),
            pltpu.SemaphoreType.DMA((18,)),
            pltpu.SemaphoreType.DMA((18,)),
            pltpu.SemaphoreType.DMA((2,)),
        ],
        compiler_params=pltpu.CompilerParams(
            collective_id=0, has_side_effects=True, vmem_limit_bytes=64 * 1000 * 1000
        ),
    )(
        feat, gain_mid.reshape(1, 256), conv_mid.reshape(27, 256, 256), down, wav, inj,
        gain_deep.reshape(1, 512), conv_deep.reshape(27, 512, 512),
    )


def solution(mesh):
    return jax.shard_map(
        functools.partial(on_device, mesh.shape["tm"], mesh.shape["rows"]),
        mesh=mesh,
        in_specs=(
            P("tm", "rows", None, None), P(), P(), P(), P("tm", None, "rows", None), P(), P(), P(),
        ),
        out_specs=P("tm", "rows", None, None),
        check_vma=False,
    )
```

time: 199 us -> 45.8 us (0.23); the launches traced: 195 us -> 45.1 us
  matrix products: 129 us -> 0 us
  Pallas kernels: 0 us -> 43.2 us
  waiting for transfers between devices: 21.7 us -> 0 us
  starting transfers between devices: 20.6 us -> 0 us
  other arithmetic: 12.2 us -> 0 us
  local copies, waits for them, and re-layouts: 10.9 us -> 1.87 us
    dot_general x63 -> x0, matrix products: 129 us -> none  [the longest x54 127 us: causal_taps(): jnp.einsum('fhwc,cd->fhwd', window, weight[depth_tap, row_tap, col_tap],...]
    pallas_call x0 -> x1, Pallas kernels: none -> 43.2 us  [on_device(): pl.pallas_call(body, out_shape=jax.ShapeDtypeStruct((2, 4, 64, 512), BF),...]
    ppermute x6 -> x0, waiting for transfers between devices: 21.7 us -> none  [the longest x2 18.6 us: passed_along(): return lax.ppermute(block, axis, route)]
    ppermute x6 -> x0, starting transfers between devices: 20.6 us -> none  [the longest x2 9.57 us: padded_2(): lax.ppermute(lax.slice_in_dim(block, 0, width, axis=dim), axis, backward)]
    reshape x1 -> x0, local copies, waits for them, and re-layouts: 5.84 us -> none  [haar_project(): level_two.astype(jnp.float32)]
    concatenate x2 -> x0, other arithmetic: 4.36 us -> none  [padded_2(): block = jnp.concatenate([low, block, high], axis=dim)]
    reduce_sum x3 -> x0, other arithmetic: 3.95 us -> none  [the longest x1 2.35 us: norm_act(): average = jnp.mean(values, axis=-1, keepdims=True)]
    slice x2 -> x0, local copies, waits for them, and re-layouts: 3.75 us -> none  [the longest x1 3.66 us: butterfly(): leading = lax.index_in_dim(blocks, 0, which_axis, keepdims=False)]
  transfers between devices with their start and end apart: 6 -> 0, of which waited for: 5 -> 0; matrix products, arithmetic and copies ran while one was open for 6% -> 0% of each run, Pallas kernels for 0% -> 0%
where the time goes in v1:
time: 45.8 us; the launch traced here: 45.1 us
  Pallas kernels  43.2 us (94%)
  local copies, waits for them, and re-layouts  1.87 us (4%)
    pallas_call x1, Pallas kernels, on_device(): pl.pallas_call(body, out_shape=jax.ShapeDtypeStruct((2, 4, 64, 512), BF),...  43.2 us
    unnamed x1, local copies, waits for them, and re-layouts  1.87 us

profile of v1, /device:TPU:70, one launch (start us, length us, event | category | flops | bytes accessed | tf_op | source)
XLA Modules:
  0.0 45.1 jit_solution(15720174785465285693)
XLA Ops:
  0.0 43.2 %shard_map.82 = bf16[2,4,64,512]{3,2,1,0:T(8,128)(2,1)} custom-call(bf16[4,8,128,256]{3,2,1,0:T(8,128)(2,1)} %refs_0_.1, f32[1,256]{1,0:T(1,128)} %bitcast.7, bf16[27,256,256]{2,1,0:T(8,128)(2,1)} %bitcast.5, bf16[8,256,512]{2,1,0:T(8,128)(2,1)} %refs_3_.1, bf16[2,24,4,64]{3,2,1,0:T(4,128)(2,1)} %refs_4_.1, bf16[24,512]{1,0:T(8,128)(2,1)} %refs_5_.1, ...), custom_call_target="tpu_custom_call" | custom-call | tf_op jit(solution)/shard_map/pallas_call | solution.py:337
  43.2 1.9 %copy.10 = bf16[2,4,64,512]{3,2,1,0:T(8,128)(2,1)} copy(bf16[2,4,64,512]{3,2,1,0:T(8,128)(2,1)} %shard_map.82) | data formatting | bytes 1048576

commit v2 on v1

--- a/solution.py
+++ b/solution.py
@@ -37,7 +37,7 @@
     n_tm, n_rows,
     feat, gain_mid, conv_mid, down, wav, inj, gain_deep, conv_deep,
     out,
-    fv, wm, wdn, wd, wv, iv, injw, wavt, xp, ym, lv, sb, fd, yp, yd, ov,
+    fv, wm, wdn, wd, wv, iv, injw, wavt, xp, ym, ye, lv, sb, fd, yp, yd, ov,
     lsem, send, recv, osem,
     *accs,
 ):
@@ -93,23 +93,25 @@
             source = sr if source is None else jnp.logical_and(source, sr)
         return target, source
 
-    def add_halo(name, src, dst, dt, dr):
+    def add_halo(name, src, dst, dt, dr, only=None):
         i = len(halo)
         desc = pltpu.make_async_remote_copy(
             src_ref=src, dst_ref=dst, send_sem=send.at[i], recv_sem=recv.at[i],
             device_id=(t_id + dt, r_id + dr), device_id_type=MESH,
         )
         target, source = both(dt, dr)
+        if only is not None:
+            target, source = jnp.logical_and(target, only), jnp.logical_and(source, only)
         halo[name] = (desc, target, source)
 
-    add_halo("u23", xp.at[4:6, 1], xp.at[4:6, 9], 0, -1)
-    add_halo("d23", xp.at[4:6, 8], xp.at[4:6, 0], 0, 1)
-    add_halo("u01", xp.at[2:4, 1], xp.at[2:4, 9], 0, -1)
-    add_halo("d01", xp.at[2:4, 8], xp.at[2:4, 0], 0, 1)
-    add_halo("z3", xp.at[5, 1:9], xp.at[1, 1:9], 1, 0)
-    add_halo("z2", xp.at[4, 1:9], xp.at[0, 1:9], 1, 0)
-    add_halo("zu", xp.at[4:6, 1], xp.at[0:2, 9], 1, -1)
-    add_halo("zd", xp.at[4:6, 8], xp.at[0:2, 0], 1, 1)
+    add_halo("u", xp.at[2:6, 1], xp.at[2:6, 9], 0, -1)
+    add_halo("d", xp.at[2:6, 8], xp.at[2:6, 0], 0, 1)
+    add_halo("ze1", xp.at[4:6, 1], xp.at[0:2, 1], 1, 0)
+    add_halo("ze8", xp.at[4:6, 8], xp.at[0:2, 8], 1, 0)
+    add_halo("z3", xp.at[5, 2:8], xp.at[1, 2:8], 1, 0)
+    add_halo("z2", xp.at[4, 2:8], xp.at[0, 2:8], 1, 0)
+    add_halo("cu", xp.at[0:2, 1], xp.at[0:2, 9], 0, -1, has_prev)
+    add_halo("cd", xp.at[0:2, 8], xp.at[0:2, 0], 0, 1, has_prev)
     for f in (1, 0):
         add_halo(f"yu{f}", yp.at[2 + f, 1], yp.at[2 + f, 5], 0, -1)
         add_halo(f"yd{f}", yp.at[2 + f, 4], yp.at[2 + f, 0], 0, 1)
@@ -144,22 +146,31 @@
 
     half_gain = gain_mid[...] * 0.5
 
-    def norm_frame(f):
+    def norm_row(f, r):
+        for piece in range(2):
+            rows = pl.ds(piece * 64, 64)
+            xp[f + 2, r + 1, rows, :] = norm_silu(fv[f, r, rows, :].astype(F32), half_gain)
+
+    for f in (3, 2, 1, 0):
         feat_loads[f].wait()
 
-        @pl.loop(0, 8)
+    @pl.loop(0, 4)
+    def _(f):
+        norm_row(f, 0)
+        norm_row(f, 7)
+
+    pl.semaphore_wait(barrier, count)
+    start("u", "d", "ze1", "ze8")
+    for f in (3, 2, 1):
+        @pl.loop(0, 3)
         def _(r):
-            for piece in range(2):
-                rows = pl.ds(piece * 64, 64)
-                xp[f + 2, r + 1, rows, :] = norm_silu(fv[f, r, rows, :].astype(F32), half_gain)
-
-    norm_frame(3)
-    norm_frame(2)
-    pl.semaphore_wait(barrier, count)
-    start("u23", "d23", "z3", "z2", "zu", "zd")
-    norm_frame(1)
-    norm_frame(0)
-    start("u01", "d01")
+            norm_row(f, 2 * r + 1)
+            norm_row(f, 2 * r + 2)
+
+        if f == 3:
+            start("z3")
+        if f == 2:
+            start("z2")
 
     injw[...] = jnp.zeros((256, 512), BF)
     wavt[...] = jnp.zeros((2, 256, 256), BF)
@@ -171,41 +182,50 @@
         for h in range(4):
             wavt[t, h * 64:(h + 1) * 64, 0:24] = coeffs[:, h, :].T.astype(BF)
 
-    def mid_block(t, first_rows, slot):
+    bands = ((2, 4), (0, 6))
+
+    def mid_block(t, band, depths, dst, base=None):
         k = 0
         for c in range(3):
-            for a in range(3):
+            for a in depths:
                 for b in range(3):
                     tap = (a * 3 + b) * 3 + c
                     for q in range(2):
                         pltpu.matmul_push_rhs(wm[tap], k % 2, q)
                         for h in range(2):
                             pltpu.matmul_acc_lhs(
-                                acc[q][c * 2 + h], xp[t + a, first_rows[q] + b + h],
+                                acc[q][c * 2 + h], xp[t + a, bands[band][q] + b + h],
                                 load_staged_rhs=k % 2 if h == 0 else None,
                             )
                     k += 1
             for q in range(2):
                 for h in range(2):
-                    ym[slot, q, h, c] = pltpu.matmul_pop(acc[q][c * 2 + h])
-
-    def mid_combine(t, first_rows, slot):
+                    total = pltpu.matmul_pop(acc[q][c * 2 + h])
+                    if base is not None:
+                        total = total + base[q, h, c]
+                    dst[q, h, c] = total
+
+    def mid_combine(t, band, src):
         for q in range(2):
             for h in range(2):
-                r = first_rows[q] + h
+                r = bands[band][q] + h
                 for n in range(2):
                     lanes = pl.ds(n * 128, 128)
-                    total = shift_down(ym[slot, q, h, 0, :, lanes]) + ym[slot, q, h, 1, :, lanes]
-                    total = total + shift_up(ym[slot, q, h, 2, :, lanes])
+                    total = shift_down(src[q, h, 0, :, lanes]) + src[q, h, 1, :, lanes]
+                    total = total + shift_up(src[q, h, 2, :, lanes])
                     level = (fv[t, r, :, lanes].astype(F32) + total).astype(BF)
                     lv[t % 2, n, r] = level.astype(F32)
 
-    inner, outer = (2, 4), (0, 6)
-
-    def mid_pair(t0, first_rows):
-        for i in range(2):
-            mid_block(t0 + i, first_rows, i)
-            mid_combine(t0 + i, first_rows, i)
+    def mid_full(t, band, slot):
+        mid_block(t, band, (0, 1, 2), ym.at[slot])
+        mid_combine(t, band, ym.at[slot])
+
+    def mid_early(t, band):
+        mid_block(t, band, (2, 1) if t == 1 else (2,), ye.at[t, band])
+
+    def mid_late(t, band, slot):
+        mid_block(t, band, (0,) if t == 1 else (1, 0), ym.at[slot], ye.at[t, band])
+        mid_combine(t, band, ym.at[slot])
 
     half_gain_deep = gain_deep[...] * 0.5
 
@@ -260,24 +280,37 @@
         start(f"yu{f}", f"yd{f}", f"yz{f}", f"yzu{f}", f"yzd{f}")
 
     ld_wm.wait()
-    mid_pair(2, inner)
-    arrive("u23", "d23", "u01", "d01")
-    mid_pair(2, outer)
+    mid_full(3, 0, 0)
+    for r in range(1, 7):
+        norm_row(0, r)
+    mid_full(2, 0, 1)
+    arrive("ze1", "ze8")
+    start("cu", "cd")
+    mid_early(1, 0)
+    mid_early(0, 0)
+    arrive("u", "d")
+    mid_full(3, 1, 0)
+    mid_full(2, 1, 1)
     ld_dn.wait()
     deep_frame(1)
     start_deep(1)
-    arrive("z3", "z2", "zu", "zd")
-    mid_pair(0, inner)
-    mid_pair(0, outer)
+    mid_early(1, 1)
+    mid_early(0, 1)
+    arrive("z3", "cu", "cd")
+    mid_late(1, 0, 0)
+    mid_late(1, 1, 1)
+    arrive("z2")
+    mid_late(0, 0, 0)
+    mid_late(0, 1, 1)
     deep_frame(0)
     start_deep(0)
 
     ld_wd.wait()
 
-    def deep_conv(t, order, waits):
+    def deep_conv(t, order, base=None):
         k = 0
-        for step, a in enumerate(order):
-            arrive(*waits[step])
+        for step, (a, names) in enumerate(order):
+            arrive(*names)
             for c in range(3):
                 for b in range(3):
                     tap = (a * 3 + b) * 3 + c
@@ -294,12 +327,14 @@
                                     load_staged_rhs=k % 2 if h == 0 else None,
                                 )
                         k += 1
-                if step == 2:
+                if step == len(order) - 1:
                     for q in range(2):
                         for h in range(2):
-                            yd[t, c, h * 128:(h + 1) * 128, q * 256:(q + 1) * 256] = (
-                                pltpu.matmul_pop(acc[q][c * 2 + h])
-                            )
+                            block = (c, slice(h * 128, (h + 1) * 128), slice(q * 256, (q + 1) * 256))
+                            total = pltpu.matmul_pop(acc[q][c * 2 + h])
+                            if base is not None:
+                                total = total + base[block]
+                            yd[(t,) + block] = total
 
     def deep_combine(t):
         for r in range(4):
@@ -310,11 +345,13 @@
                 total = total + shift_up(yd[t, 2, rows, lanes])
                 ov[t, r, :, lanes] = (fd[t, rows, lanes] + total).astype(BF)
 
-    deep_conv(1, (2, 0, 1), (("yu1", "yd1"), ("yz1", "yzu1", "yzd1"), ("yu0", "yd0")))
+    arrive("yu1", "yd1", "yz1", "yzu1", "yzd1")
+    deep_conv(0, ((1, ()),))
+    deep_conv(1, ((2, ()), (0, ()), (1, ("yu0", "yd0"))))
     deep_combine(1)
     store1 = pltpu.make_async_copy(ov.at[1], out.at[1], osem.at[1])
     store1.start()
-    deep_conv(0, (1, 2, 0), ((), (), ("yz0", "yzu0", "yzd0")))
+    deep_conv(0, ((2, ()), (0, ("yz0", "yzu0", "yzd0"))), yd.at[0])
     deep_combine(0)
     store0 = pltpu.make_async_copy(ov.at[0], out.at[0], osem.at[0])
     store0.start()
@@ -350,6 +387,7 @@
             pltpu.VMEM((2, 256, 256), BF),
             pltpu.VMEM((6, 10, 128, 256), BF),
             pltpu.VMEM((2, 2, 2, 3, 128, 256), F32),
+            pltpu.VMEM((2, 2, 2, 2, 3, 128, 256), F32),
             pltpu.VMEM((2, 2, 8, 128, 128), F32),
             pltpu.VMEM((8, 256, 256), BF),
             pltpu.VMEM((2, 256, 512), F32),

time: 45.8 us -> 39.2 us (0.86); the launches traced: 45.1 us -> 39.1 us
  Pallas kernels: 43.2 us -> 37.2 us
    pallas_call x1, Pallas kernels: 43.2 us -> 37.2 us  [on_device(): pl.pallas_call(body, out_shape=jax.ShapeDtypeStruct((2, 4, 64, 512), BF),...]
where the time goes in v2:
time: 39.2 us; the launch traced here: 39.1 us
  Pallas kernels  37.2 us (95%)
  local copies, waits for them, and re-layouts  1.87 us (5%)
    pallas_call x1, Pallas kernels, on_device(): pl.pallas_call(body, out_shape=jax.ShapeDtypeStruct((2, 4, 64, 512), BF),...  37.2 us
    unnamed x1, local copies, waits for them, and re-layouts  1.87 us

profile of v2, /device:TPU:70, one launch (start us, length us, event | category | flops | bytes accessed | tf_op | source)
XLA Modules:
  0.0 39.1 jit_solution(5724029033723479387)
XLA Ops:
  0.0 37.2 %shard_map.82 = bf16[2,4,64,512]{3,2,1,0:T(8,128)(2,1)} custom-call(bf16[4,8,128,256]{3,2,1,0:T(8,128)(2,1)} %refs_0_.1, f32[1,256]{1,0:T(1,128)} %bitcast.7, bf16[27,256,256]{2,1,0:T(8,128)(2,1)} %bitcast.5, bf16[8,256,512]{2,1,0:T(8,128)(2,1)} %refs_3_.1, bf16[2,24,4,64]{3,2,1,0:T(4,128)(2,1)} %refs_4_.1, bf16[24,512]{1,0:T(8,128)(2,1)} %refs_5_.1, ...), custom_call_target="tpu_custom_call" | custom-call | tf_op jit(solution)/shard_map/pallas_call | solution.py:374
  37.2 1.9 %copy.10 = bf16[2,4,64,512]{3,2,1,0:T(8,128)(2,1)} copy(bf16[2,4,64,512]{3,2,1,0:T(8,128)(2,1)} %shard_map.82) | data formatting | bytes 1048576

commit v3 on v2

--- a/solution.py
+++ b/solution.py
@@ -37,14 +37,14 @@
     n_tm, n_rows,
     feat, gain_mid, conv_mid, down, wav, inj, gain_deep, conv_deep,
     out,
-    fv, wm, wdn, wd, wv, iv, injw, wavt, xp, ym, ye, lv, sb, fd, yp, yd, ov,
-    lsem, send, recv, osem,
+    fv, wm, wdn, wd, wv, iv, injw, wavt, xp, xv, um, ym, pe, lv, sb, fd, yp, yd,
+    lsem, send, recv,
     *accs,
 ):
     t_id, r_id = lax.axis_index("tm"), lax.axis_index("rows")
     has_prev, has_next = t_id > 0, t_id < n_tm - 1
     has_up, has_dn = r_id > 0, r_id < n_rows - 1
-    acc = (accs[:6], accs[6:])
+    acc = (accs[:8], accs[8:])
 
     def load(i, src, dst):
         return pltpu.make_async_copy(src, dst, lsem.at[i])
@@ -182,50 +182,87 @@
         for h in range(4):
             wavt[t, h * 64:(h + 1) * 64, 0:24] = coeffs[:, h, :].T.astype(BF)
 
-    bands = ((2, 4), (0, 6))
-
-    def mid_block(t, band, depths, dst, base=None):
-        k = 0
+    bands = ((1, 2), (0, 3))
+
+    def weight_rows(a, c):
+        for piece in range(4):
+            rows = pl.ds(piece * 64, 64)
+            g = [wm[(a * 3 + b) * 3 + c, rows, :].astype(F32) for b in range(3)]
+            side = g[0] + g[2]
+            um[a, c, 0, rows, :] = ((side + g[1]) * 0.5).astype(BF)
+            um[a, c, 1, rows, :] = ((side - g[1]) * 0.5).astype(BF)
+
+    def data_rows(f, p):
+        for piece in range(4):
+            rows = pl.ds(piece * 32, 32)
+            d = [xp[f, 2 * p + j, rows, :] for j in range(4)]
+            xv[f, p, 0, rows, :] = d[0] - d[2]
+            xv[f, p, 1, rows, :] = d[1] + d[2]
+            xv[f, p, 2, rows, :] = d[2] - d[1]
+            xv[f, p, 3, rows, :] = d[1] - d[3]
+
+    def data_band(f, band):
+        for p in bands[band]:
+            data_rows(f, p)
+
+    def mid_weight(i, a, c):
+        if i == 0:
+            return wm[a * 9 + c]
+        if i == 3:
+            return wm[a * 9 + 6 + c]
+        return um[a, c, i - 1]
+
+    def mid_block(t, band, depths, slot):
         for c in range(3):
-            for a in depths:
-                for b in range(3):
-                    tap = (a * 3 + b) * 3 + c
+            base = 4 * (c % 2)
+            k = 0
+            for e in range(2):
+                for a in depths:
                     for q in range(2):
-                        pltpu.matmul_push_rhs(wm[tap], k % 2, q)
+                        i = 2 * q + e
+                        pltpu.matmul_push_rhs(mid_weight(i, a, c), k % 2, q)
                         for h in range(2):
                             pltpu.matmul_acc_lhs(
-                                acc[q][c * 2 + h], xp[t + a, bands[band][q] + b + h],
+                                acc[q][base + e * 2 + h], xv[t + a, bands[band][h], i],
                                 load_staged_rhs=k % 2 if h == 0 else None,
                             )
                     k += 1
-            for q in range(2):
-                for h in range(2):
-                    total = pltpu.matmul_pop(acc[q][c * 2 + h])
-                    if base is not None:
-                        total = total + base[q, h, c]
-                    dst[q, h, c] = total
-
-    def mid_combine(t, band, src):
-        for q in range(2):
-            for h in range(2):
-                r = bands[band][q] + h
-                for n in range(2):
-                    lanes = pl.ds(n * 128, 128)
-                    total = shift_down(src[q, h, 0, :, lanes]) + src[q, h, 1, :, lanes]
-                    total = total + shift_up(src[q, h, 2, :, lanes])
-                    level = (fv[t, r, :, lanes].astype(F32) + total).astype(BF)
-                    lv[t % 2, n, r] = level.astype(F32)
+                for q in range(2):
+                    for h in range(2):
+                        ym[slot, h, c, 2 * q + e] = pltpu.matmul_pop(acc[q][base + e * 2 + h])
+
+    def mid_combine(t, band, slot, early=False, late=False):
+        for h in range(2):
+            p = bands[band][h]
+            for n in range(2):
+                lanes = pl.ds(n * 128, 128)
+                pair = ([], [])
+                for c in range(3):
+                    m = [ym[slot, h, c, i, :, lanes] for i in range(4)]
+                    pair[0].append(m[0] + (m[1] + m[2]))
+                    pair[1].append((m[1] - m[2]) - m[3])
+                for j in range(2):
+                    r = 2 * p + j
+                    total = shift_down(pair[j][0]) + pair[j][1] + shift_up(pair[j][2])
+                    if late:
+                        total = total + pe[t, r, :, lanes]
+                    if early:
+                        pe[t, r, :, lanes] = total
+                    else:
+                        level = (fv[t, r, :, lanes].astype(F32) + total).astype(BF)
+                        lv[t % 2, n, r] = level.astype(F32)
 
     def mid_full(t, band, slot):
-        mid_block(t, band, (0, 1, 2), ym.at[slot])
-        mid_combine(t, band, ym.at[slot])
-
-    def mid_early(t, band):
-        mid_block(t, band, (2, 1) if t == 1 else (2,), ye.at[t, band])
+        mid_block(t, band, (0, 1, 2), slot)
+        mid_combine(t, band, slot)
+
+    def mid_early(t, band, slot):
+        mid_block(t, band, (2, 1) if t == 1 else (2,), slot)
+        mid_combine(t, band, slot, early=True)
 
     def mid_late(t, band, slot):
-        mid_block(t, band, (0,) if t == 1 else (1, 0), ym.at[slot], ye.at[t, band])
-        mid_combine(t, band, ym.at[slot])
+        mid_block(t, band, (0,) if t == 1 else (1, 0), slot)
+        mid_combine(t, band, slot, late=True)
 
     half_gain_deep = gain_deep[...] * 0.5
 
@@ -280,26 +317,38 @@
         start(f"yu{f}", f"yd{f}", f"yz{f}", f"yzu{f}", f"yzd{f}")
 
     ld_wm.wait()
+    for c in range(3):
+        for a in range(3):
+            weight_rows(a, c)
+    for f in (3, 4, 5):
+        data_band(f, 0)
     mid_full(3, 0, 0)
     for r in range(1, 7):
         norm_row(0, r)
+    data_band(2, 0)
     mid_full(2, 0, 1)
     arrive("ze1", "ze8")
     start("cu", "cd")
-    mid_early(1, 0)
-    mid_early(0, 0)
+    mid_early(1, 0, 0)
+    mid_early(0, 0, 1)
     arrive("u", "d")
+    for f in (3, 4, 5, 2):
+        data_band(f, 1)
     mid_full(3, 1, 0)
     mid_full(2, 1, 1)
     ld_dn.wait()
     deep_frame(1)
     start_deep(1)
-    mid_early(1, 1)
-    mid_early(0, 1)
+    mid_early(1, 1, 0)
+    mid_early(0, 1, 1)
     arrive("z3", "cu", "cd")
+    data_band(1, 0)
+    data_band(1, 1)
     mid_late(1, 0, 0)
     mid_late(1, 1, 1)
     arrive("z2")
+    data_band(0, 0)
+    data_band(0, 1)
     mid_late(0, 0, 0)
     mid_late(0, 1, 1)
     deep_frame(0)
@@ -343,23 +392,17 @@
                 lanes = slice(n * 128, (n + 1) * 128)
                 total = shift_down(yd[t, 0, rows, lanes]) + yd[t, 1, rows, lanes]
                 total = total + shift_up(yd[t, 2, rows, lanes])
-                ov[t, r, :, lanes] = (fd[t, rows, lanes] + total).astype(BF)
+                out[t, r, :, lanes] = (fd[t, rows, lanes] + total).astype(BF)
 
     arrive("yu1", "yd1", "yz1", "yzu1", "yzd1")
     deep_conv(0, ((1, ()),))
     deep_conv(1, ((2, ()), (0, ()), (1, ("yu0", "yd0"))))
     deep_combine(1)
-    store1 = pltpu.make_async_copy(ov.at[1], out.at[1], osem.at[1])
-    store1.start()
     deep_conv(0, ((2, ()), (0, ("yz0", "yzu0", "yzd0"))), yd.at[0])
     deep_combine(0)
-    store0 = pltpu.make_async_copy(ov.at[0], out.at[0], osem.at[0])
-    store0.start()
 
     for desc, target, _ in halo.values():
         pl.when(target)(desc.wait_send)
-    store1.wait()
-    store0.wait()
 
 
 def on_device(n_tm, n_rows, feat, gain_mid, conv_mid, down, wav, inj, gain_deep, conv_deep):
@@ -367,15 +410,15 @@
         def inner(*accs):
             kernel(n_tm, n_rows, *refs, *accs)
 
-        pl.run_scoped(inner, *[pltpu.ACC(q)((128, 256), F32) for q in range(2) for _ in range(6)])
-
-    hbm = pl.BlockSpec(memory_space=pl.ANY)
+        pl.run_scoped(inner, *[pltpu.ACC(q)((128, 256), F32) for q in range(2) for _ in range(8)])
+
+    hbm = pl.BlockSpec(memory_space=pltpu.HBM)
     vmem = pl.BlockSpec(memory_space=pltpu.VMEM)
     return pl.pallas_call(
         body,
-        out_shape=jax.ShapeDtypeStruct((2, 4, 64, 512), BF),
+        out_shape=pltpu.VMEM((2, 4, 64, 512), BF),
         in_specs=[hbm, vmem, hbm, hbm, hbm, hbm, vmem, hbm],
-        out_specs=hbm,
+        out_specs=vmem,
         scratch_shapes=[
             pltpu.VMEM((4, 8, 128, 256), BF),
             pltpu.VMEM((27, 256, 256), BF),
@@ -386,26 +429,29 @@
             pltpu.VMEM((256, 512), BF),
             pltpu.VMEM((2, 256, 256), BF),
             pltpu.VMEM((6, 10, 128, 256), BF),
-            pltpu.VMEM((2, 2, 2, 3, 128, 256), F32),
-            pltpu.VMEM((2, 2, 2, 2, 3, 128, 256), F32),
+            pltpu.VMEM((6, 4, 4, 128, 256), BF),
+            pltpu.VMEM((3, 3, 2, 256, 256), BF),
+            pltpu.VMEM((2, 2, 3, 4, 128, 256), F32),
+            pltpu.VMEM((2, 8, 128, 256), F32),
             pltpu.VMEM((2, 2, 8, 128, 128), F32),
             pltpu.VMEM((8, 256, 256), BF),
             pltpu.VMEM((2, 256, 512), F32),
             pltpu.VMEM((4, 6, 64, 512), BF),
             pltpu.VMEM((2, 3, 256, 512), F32),
-            pltpu.VMEM((2, 4, 64, 512), BF),
             pltpu.SemaphoreType.DMA((9,)),
             pltpu.SemaphoreType.DMA((18,)),
             pltpu.SemaphoreType.DMA((18,)),
-            pltpu.SemaphoreType.DMA((2,)),
         ],
         compiler_params=pltpu.CompilerParams(
-            collective_id=0, has_side_effects=True, vmem_limit_bytes=64 * 1000 * 1000
+            collective_id=0, has_side_effects=True, vmem_limit_bytes=60 * 1000 * 1000
         ),
-    )(
-        feat, gain_mid.reshape(1, 256), conv_mid.reshape(27, 256, 256), down, wav, inj,
-        gain_deep.reshape(1, 512), conv_deep.reshape(27, 512, 512),
-    )
+    )(*[
+        pltpu.with_memory_space_constraint(x, pltpu.HBM)
+        for x in (
+            feat, gain_mid.reshape(1, 256), conv_mid.reshape(27, 256, 256), down, wav, inj,
+            gain_deep.reshape(1, 512), conv_deep.reshape(27, 512, 512),
+        )
+    ])
 
 
 def solution(mesh):

time: 39.2 us -> 35 us (0.89)
  Pallas kernels: 37.2 us -> 34.1 us
  local copies, waits for them, and re-layouts: 1.87 us -> 0.8 us
    pallas_call x1, Pallas kernels: 37.2 us -> 34.1 us  [on_device(): pl.pallas_call(body, out_shape=pltpu.VMEM((2, 4, 64, 512), BF), in_specs=...]
    unnamed x1, local copies, waits for them, and re-layouts: 1.87 us -> 0.8 us
where the time goes in v3:
time: 35 us; the launch traced here: 34.9 us
  Pallas kernels  34.1 us (97%)
  local copies, waits for them, and re-layouts  0.8 us (2%)
    pallas_call x1, Pallas kernels, on_device(): pl.pallas_call(body, out_shape=pltpu.VMEM((2, 4, 64, 512), BF), in_specs=...  34.1 us
    unnamed x1, local copies, waits for them, and re-layouts  0.8 us

profile of v3, /device:TPU:70, one launch (start us, length us, event | category | flops | bytes accessed | tf_op | source)
XLA Modules:
  0.0 34.9 jit_solution(10705954021765098831)
XLA Ops:
  0.0 34.1 %shard_map.82 = bf16[2,4,64,512]{3,2,1,0:T(8,128)(2,1)S(1)} custom-call(bf16[4,8,128,256]{3,2,1,0:T(8,128)(2,1)} %refs_0_.1, f32[1,256]{1,0:T(1,128)} %bitcast.7, bf16[27,256,256]{2,1,0:T(8,128)(2,1)} %bitcast.5, bf16[8,256,512]{2,1,0:T(8,128)(2,1)} %refs_3_.1, bf16[2,24,4,64]{3,2,1,0:T(4,128)(2,1)} %refs_4_.1, bf16[24,512]{1,0:T(8,128)(2,1)} %refs_5_.1, ...), custom_call_target="tpu_custom_call" | custom-call | tf_op jit(solution)/shard_map/pallas_call | solution.py:417
  34.1 0.8 %copy.10 = bf16[2,4,64,512]{3,2,1,0:T(8,128)(2,1)} copy(bf16[2,4,64,512]{3,2,1,0:T(8,128)(2,1)S(1)} %shard_map.82) | data formatting | bytes 1048576

commit v4 on v3

--- a/solution.py
+++ b/solution.py
@@ -23,21 +23,23 @@
 
 
 def shift_down(x):
-    row = lax.broadcasted_iota(jnp.int32, x.shape, 0)
-    return jnp.where(row == 0, 0.0, pltpu.roll(x, 1, 0))
+    moved = pltpu.roll(x, 1, 0)
+    row = lax.broadcasted_iota(jnp.int32, (8, x.shape[1]), 0)
+    return jnp.concatenate([jnp.where(row == 0, 0.0, moved[:8]), moved[8:]], axis=0)
 
 
 def shift_up(x):
     n = x.shape[0]
-    row = lax.broadcasted_iota(jnp.int32, x.shape, 0)
-    return jnp.where(row == n - 1, 0.0, pltpu.roll(x, n - 1, 0))
+    moved = pltpu.roll(x, n - 1, 0)
+    row = lax.broadcasted_iota(jnp.int32, (8, x.shape[1]), 0)
+    return jnp.concatenate([moved[:n - 8], jnp.where(row == 7, 0.0, moved[n - 8:])], axis=0)
 
 
 def kernel(
     n_tm, n_rows,
     feat, gain_mid, conv_mid, down, wav, inj, gain_deep, conv_deep,
     out,
-    fv, wm, wdn, wd, wv, iv, injw, wavt, xp, xv, um, ym, pe, lv, sb, fd, yp, yd,
+    fv, wm, wdn, wd, wv, iv, injw, wavt, xp, xv, um, ym0, ym1, pe, ff, lv, sb, fd, yp, yd0, yd1,
     lsem, send, recv,
     *accs,
 ):
@@ -45,6 +47,8 @@
     has_prev, has_next = t_id > 0, t_id < n_tm - 1
     has_up, has_dn = r_id > 0, r_id < n_rows - 1
     acc = (accs[:8], accs[8:])
+    ym = (ym0, ym1)
+    yd = (yd0, yd1)
 
     def load(i, src, dst):
         return pltpu.make_async_copy(src, dst, lsem.at[i])
@@ -104,8 +108,10 @@
             target, source = jnp.logical_and(target, only), jnp.logical_and(source, only)
         halo[name] = (desc, target, source)
 
-    add_halo("u", xp.at[2:6, 1], xp.at[2:6, 9], 0, -1)
-    add_halo("d", xp.at[2:6, 8], xp.at[2:6, 0], 0, 1)
+    add_halo("u", xp.at[3:6, 1], xp.at[3:6, 9], 0, -1)
+    add_halo("d", xp.at[3:6, 8], xp.at[3:6, 0], 0, 1)
+    add_halo("u0", xp.at[2, 1], xp.at[2, 9], 0, -1)
+    add_halo("d0", xp.at[2, 8], xp.at[2, 0], 0, 1)
     add_halo("ze1", xp.at[4:6, 1], xp.at[0:2, 1], 1, 0)
     add_halo("ze8", xp.at[4:6, 8], xp.at[0:2, 8], 1, 0)
     add_halo("z3", xp.at[5, 2:8], xp.at[1, 2:8], 1, 0)
@@ -144,12 +150,19 @@
         xp[:, 9] = jnp.zeros((6, 128, 256), BF)
         yp[:, 5] = jnp.zeros((4, 64, 512), BF)
 
+    for slot in range(2):
+        for end in (0, 136):
+            ym[slot][:, :, :, :, end:end + 8, :] = jnp.zeros((2, 3, 4, 2, 8, 128), F32)
+
     half_gain = gain_mid[...] * 0.5
 
     def norm_row(f, r):
         for piece in range(2):
             rows = pl.ds(piece * 64, 64)
-            xp[f + 2, r + 1, rows, :] = norm_silu(fv[f, r, rows, :].astype(F32), half_gain)
+            x = fv[f, r, rows, :].astype(F32)
+            xp[f + 2, r + 1, rows, :] = norm_silu(x, half_gain)
+            for n in range(2):
+                ff[f, r, n, rows, :] = x[:, n * 128:(n + 1) * 128]
 
     for f in (3, 2, 1, 0):
         feat_loads[f].wait()
@@ -160,7 +173,7 @@
         norm_row(f, 7)
 
     pl.semaphore_wait(barrier, count)
-    start("u", "d", "ze1", "ze8")
+    start("u", "d", "ze1", "ze8", "u0", "d0")
     for f in (3, 2, 1):
         @pl.loop(0, 3)
         def _(r):
@@ -187,10 +200,10 @@
     def weight_rows(a, c):
         for piece in range(4):
             rows = pl.ds(piece * 64, 64)
-            g = [wm[(a * 3 + b) * 3 + c, rows, :].astype(F32) for b in range(3)]
+            g = [wm[(a * 3 + b) * 3 + c, rows, :] for b in range(3)]
             side = g[0] + g[2]
-            um[a, c, 0, rows, :] = ((side + g[1]) * 0.5).astype(BF)
-            um[a, c, 1, rows, :] = ((side - g[1]) * 0.5).astype(BF)
+            um[a, c, 0, rows, :] = (side + g[1]) * jnp.bfloat16(0.5)
+            um[a, c, 1, rows, :] = (side - g[1]) * jnp.bfloat16(0.5)
 
     def data_rows(f, p):
         for piece in range(4):
@@ -229,46 +242,65 @@
                     k += 1
                 for q in range(2):
                     for h in range(2):
-                        ym[slot, h, c, 2 * q + e] = pltpu.matmul_pop(acc[q][base + e * 2 + h])
+                        product = pltpu.matmul_pop(acc[q][base + e * 2 + h])
+                        for n in range(2):
+                            ym[slot][h, c, 2 * q + e, n, 8:136, :] = product[:, n * 128:(n + 1) * 128]
 
     def mid_combine(t, band, slot, early=False, late=False):
         for h in range(2):
             p = bands[band][h]
             for n in range(2):
-                lanes = pl.ds(n * 128, 128)
-                pair = ([], [])
-                for c in range(3):
-                    m = [ym[slot, h, c, i, :, lanes] for i in range(4)]
-                    pair[0].append(m[0] + (m[1] + m[2]))
-                    pair[1].append((m[1] - m[2]) - m[3])
-                for j in range(2):
-                    r = 2 * p + j
-                    total = shift_down(pair[j][0]) + pair[j][1] + shift_up(pair[j][2])
-                    if late:
-                        total = total + pe[t, r, :, lanes]
-                    if early:
-                        pe[t, r, :, lanes] = total
-                    else:
-                        level = (fv[t, r, :, lanes].astype(F32) + total).astype(BF)
-                        lv[t % 2, n, r] = level.astype(F32)
-
-    def mid_full(t, band, slot):
-        mid_block(t, band, (0, 1, 2), slot)
-        mid_combine(t, band, slot)
-
-    def mid_early(t, band, slot):
-        mid_block(t, band, (2, 1) if t == 1 else (2,), slot)
-        mid_combine(t, band, slot, early=True)
-
-    def mid_late(t, band, slot):
-        mid_block(t, band, (0,) if t == 1 else (1, 0), slot)
-        mid_combine(t, band, slot, late=True)
+                for odd in range(2):
+                    for piece in range(4):
+                        z = []
+                        for i in range(4):
+                            terms = [
+                                ym[slot][h, c, i, n, pl.ds(7 + c + odd + 32 * piece, 16, stride=2), :]
+                                for c in range(3)
+                            ]
+                            z.append(terms[0] + terms[1] + terms[2])
+                        pair = (z[0] + (z[1] + z[2]), (z[1] - z[2]) - z[3])
+                        place = pl.ds(16 * piece, 16)
+                        for j in range(2):
+                            r = 2 * p + j
+                            total = pair[j]
+                            if late:
+                                total = total + pe[t, n, r, odd, place, :]
+                            else:
+                                total = total + ff[t, r, n, pl.ds(odd + 32 * piece, 16, stride=2), :]
+                            if early:
+                                pe[t, n, r, odd, place, :] = total
+                            else:
+                                lv[t % 2, n, r, odd, place, :] = total.astype(BF).astype(F32)
+
+    pending = []
+
+    def flush():
+        while pending:
+            pending.pop(0)()
+
+    def mid_step(t, band, depths, **kind):
+        slot = mid_step.count % 2
+        mid_step.count += 1
+        mid_block(t, band, depths, slot)
+        flush()
+        pending.append(lambda: mid_combine(t, band, slot, **kind))
+
+    mid_step.count = 0
+
+    def mid_full(t, band):
+        mid_step(t, band, (0, 1, 2))
+
+    def mid_early(t, band):
+        mid_step(t, band, (2, 1) if t == 1 else (2,), early=True)
+
+    def mid_late(t, band):
+        mid_step(t, band, (0,) if t == 1 else (1, 0), late=True)
 
     half_gain_deep = gain_deep[...] * 0.5
 
-    def deep_frame(t):
-        @pl.loop(0, 4)
-        def _(r):
+    def haar(t):
+        for r in range(4):
             for piece in range(4):
                 for n in range(2):
                     lanes = pl.ds(n * 128, 128)
@@ -277,7 +309,7 @@
                         for j in range(2):
                             for k in range(2):
                                 v[i, j, k] = lv[
-                                    i, n, 2 * r + j, pl.ds(piece * 32 + k, 16, stride=2), :
+                                    i, n, 2 * r + j, k, pl.ds(piece * 16, 16), :
                                 ]
                     for axis in range(3):
                         w = {}
@@ -291,9 +323,10 @@
                         for j in range(2):
                             for k in range(2):
                                 s = 4 * i + 2 * j + k
-                                row = pl.multiple_of(r * 64 + piece * 16, 16)
+                                row = r * 64 + piece * 16
                                 sb[s, pl.ds(row, 16), lanes] = (v[i, j, k] * haar_scale).astype(BF)
 
+    def project(t):
         for s in range(9):
             for q in range(2):
                 cols = slice(q * 256, (q + 1) * 256)
@@ -307,10 +340,10 @@
             for q in range(2):
                 fd[t, h * 128:(h + 1) * 128, q * 256:(q + 1) * 256] = pltpu.matmul_pop(acc[q][h])
 
-        @pl.loop(0, 4)
-        def _(r):
+    def deep_norm(t):
+        for r in range(4):
             for piece in range(2):
-                rows = pl.ds(pl.multiple_of(r * 64 + piece * 32, 32), 32)
+                rows = pl.ds(r * 64 + piece * 32, 32)
                 yp[t + 2, r + 1, pl.ds(piece * 32, 32), :] = norm_silu(fd[t, rows, :], half_gain_deep)
 
     def start_deep(f):
@@ -322,40 +355,6 @@
             weight_rows(a, c)
     for f in (3, 4, 5):
         data_band(f, 0)
-    mid_full(3, 0, 0)
-    for r in range(1, 7):
-        norm_row(0, r)
-    data_band(2, 0)
-    mid_full(2, 0, 1)
-    arrive("ze1", "ze8")
-    start("cu", "cd")
-    mid_early(1, 0, 0)
-    mid_early(0, 0, 1)
-    arrive("u", "d")
-    for f in (3, 4, 5, 2):
-        data_band(f, 1)
-    mid_full(3, 1, 0)
-    mid_full(2, 1, 1)
-    ld_dn.wait()
-    deep_frame(1)
-    start_deep(1)
-    mid_early(1, 1, 0)
-    mid_early(0, 1, 1)
-    arrive("z3", "cu", "cd")
-    data_band(1, 0)
-    data_band(1, 1)
-    mid_late(1, 0, 0)
-    mid_late(1, 1, 1)
-    arrive("z2")
-    data_band(0, 0)
-    data_band(0, 1)
-    mid_late(0, 0, 0)
-    mid_late(0, 1, 1)
-    deep_frame(0)
-    start_deep(0)
-
-    ld_wd.wait()
-
     def deep_conv(t, order, base=None):
         k = 0
         for step, (a, names) in enumerate(order):
@@ -383,22 +382,61 @@
                             total = pltpu.matmul_pop(acc[q][c * 2 + h])
                             if base is not None:
                                 total = total + base[block]
-                            yd[(t,) + block] = total
+                            yd[t][block] = total
 
     def deep_combine(t):
         for r in range(4):
             rows = slice(r * 64, (r + 1) * 64)
             for n in range(4):
                 lanes = slice(n * 128, (n + 1) * 128)
-                total = shift_down(yd[t, 0, rows, lanes]) + yd[t, 1, rows, lanes]
-                total = total + shift_up(yd[t, 2, rows, lanes])
+                total = shift_down(yd[t][0, rows, lanes]) + yd[t][1, rows, lanes]
+                total = total + shift_up(yd[t][2, rows, lanes])
                 out[t, r, :, lanes] = (fd[t, rows, lanes] + total).astype(BF)
 
+    mid_full(3, 0)
+    for r in range(1, 7):
+        norm_row(0, r)
+    data_band(2, 0)
+    mid_full(2, 0)
+    arrive("ze1", "ze8")
+    start("cu", "cd")
+    mid_early(1, 0)
+    mid_early(0, 0)
+    arrive("u", "d")
+    for f in (3, 4, 5):
+        data_band(f, 1)
+    mid_full(3, 1)
+    arrive("u0", "d0")
+    data_band(2, 1)
+    mid_full(2, 1)
+    mid_early(1, 1)
+    ld_dn.wait()
+    haar(1)
+    project(1)
+    deep_norm(1)
+    start_deep(1)
+    mid_early(0, 1)
+    arrive("z3", "cu", "cd")
+    data_band(1, 0)
+    data_band(1, 1)
+    mid_late(1, 0)
+    mid_late(1, 1)
+    arrive("z2")
+    data_band(0, 0)
+    data_band(0, 1)
+    mid_late(0, 0)
+    mid_late(0, 1)
+    flush()
+    haar(0)
+    project(0)
+    deep_norm(0)
+    start_deep(0)
+    ld_wd.wait()
     arrive("yu1", "yd1", "yz1", "yzu1", "yzd1")
     deep_conv(0, ((1, ()),))
     deep_conv(1, ((2, ()), (0, ()), (1, ("yu0", "yd0"))))
     deep_combine(1)
-    deep_conv(0, ((2, ()), (0, ("yz0", "yzu0", "yzd0"))), yd.at[0])
+    deep_conv(0, ((2, ()), (0, ("yz0", "yzu0", "yzd0"))), yd0)
     deep_combine(0)
 
     for desc, target, _ in halo.values():
@@ -431,19 +469,22 @@
             pltpu.VMEM((6, 10, 128, 256), BF),
             pltpu.VMEM((6, 4, 4, 128, 256), BF),
             pltpu.VMEM((3, 3, 2, 256, 256), BF),
-            pltpu.VMEM((2, 2, 3, 4, 128, 256), F32),
-            pltpu.VMEM((2, 8, 128, 256), F32),
-            pltpu.VMEM((2, 2, 8, 128, 128), F32),
+            pltpu.VMEM((2, 3, 4, 2, 144, 128), F32),
+            pltpu.VMEM((2, 3, 4, 2, 144, 128), F32),
+            pltpu.VMEM((2, 2, 8, 2, 64, 128), F32),
+            pltpu.VMEM((4, 8, 2, 128, 128), F32),
+            pltpu.VMEM((2, 2, 8, 2, 64, 128), F32),
             pltpu.VMEM((8, 256, 256), BF),
             pltpu.VMEM((2, 256, 512), F32),
             pltpu.VMEM((4, 6, 64, 512), BF),
-            pltpu.VMEM((2, 3, 256, 512), F32),
+            pltpu.VMEM((3, 256, 512), F32),
+            pltpu.VMEM((3, 256, 512), F32),
             pltpu.SemaphoreType.DMA((9,)),
-            pltpu.SemaphoreType.DMA((18,)),
-            pltpu.SemaphoreType.DMA((18,)),
+            pltpu.SemaphoreType.DMA((20,)),
+            pltpu.SemaphoreType.DMA((20,)),
         ],
         compiler_params=pltpu.CompilerParams(
-            collective_id=0, has_side_effects=True, vmem_limit_bytes=60 * 1000 * 1000
+            collective_id=0, has_side_effects=True, vmem_limit_bytes=63 * 1000 * 1000
         ),
     )(*[
         pltpu.with_memory_space_constraint(x, pltpu.HBM)

time: 35 us -> 34 us (0.971)
  the two profiles are of different devices: /device:TPU:70 before, /device:TPU:39 now
where the time goes in v4:
time: 34 us; the launch traced here: 33.9 us
  Pallas kernels  33.1 us (97%)
  local copies, waits for them, and re-layouts  0.8 us (2%)
    pallas_call x1, Pallas kernels, on_device(): pl.pallas_call(body, out_shape=pltpu.VMEM((2, 4, 64, 512), BF), in_specs=...  33.1 us
    unnamed x1, local copies, waits for them, and re-layouts  0.8 us

profile of v4, /device:TPU:39, one launch (start us, length us, event | category | flops | bytes accessed | tf_op | source)
XLA Modules:
  0.0 33.9 jit_solution(2336944038101067816)
XLA Ops:
  0.0 33.1 %shard_map.82 = bf16[2,4,64,512]{3,2,1,0:T(8,128)(2,1)S(1)} custom-call(bf16[4,8,128,256]{3,2,1,0:T(8,128)(2,1)} %refs_0_.1, f32[1,256]{1,0:T(1,128)} %bitcast.7, bf16[27,256,256]{2,1,0:T(8,128)(2,1)} %bitcast.5, bf16[8,256,512]{2,1,0:T(8,128)(2,1)} %refs_3_.1, bf16[2,24,4,64]{3,2,1,0:T(4,128)(2,1)} %refs_4_.1, bf16[24,512]{1,0:T(8,128)(2,1)} %refs_5_.1, ...), custom_call_target="tpu_custom_call" | custom-call | tf_op jit(solution)/shard_map/pallas_call | solution.py:455
  33.1 0.8 %copy.10 = bf16[2,4,64,512]{3,2,1,0:T(8,128)(2,1)} copy(bf16[2,4,64,512]{3,2,1,0:T(8,128)(2,1)S(1)} %shard_map.82) | data formatting | bytes 1048576
